TPU v7x, 32 devices: a whole 2x2x4 slice. The times are simulated.
32 devices in a mesh: section: 2 (over y), row: 4 (over x, core), col: 4 (over z).
Axes of the slice: x: 2, y: 2, z: 4, core: 2. Of those that a mesh axis runs over, the one named last changes fastest.
Arguments:
- inputs: float32 [3, 128, 16384], P(None, None, ('row', 'col')), may hold values from -512 to 512
- weights: float32 [2, 4, 4, 1024, 16384], P('section', None, 'col', None, 'row'), may hold values from -1 to 1
- norm_gain: float32 [2, 16384], P('section', ('row', 'col')), may hold values from 0.5 to 1.5
Outputs:
- section_outputs: float32 [2, 3, 128, 16384], P('section', None, None, ('row', 'col'))
All inputs are finite; a program needn't handle non-finite values.
Results may differ from a plain program's by a relative error of at most 0.00036.
Values sent between devices are 32-bit elements; how exact they have to be, the bound alone decides.
A program may use at most 192 MiB of HBM per device.

v0:
```python
import jax
import jax.numpy as jnp
from jax import lax
from jax.sharding import PartitionSpec as P


def from_behind(value, axis, steps):
    count = lax.axis_size(axis)
    initial, last = (max(0, -steps), min(count, count - steps))
    return lax.ppermute(value, axis, [(source, source + steps) for source in range(initial, last)])


def split_two(values):
    first = lax.optimization_barrier(values.astype(jnp.bfloat16))
    second = lax.optimization_barrier((values - first.astype(jnp.float32)).astype(jnp.bfloat16))
    return (first, second)


def shards(inputs, weights, norm_gain):
    section_id = lax.axis_index("section")
    row_count = lax.axis_size("row")
    pieces = weights.shape[3]
    out_cols = weights.shape[4]
    flat = weights.reshape(row_count * pieces, out_cols)
    wfirst, wsecond = split_two(flat)
    micro = inputs.shape[0]
    rows = inputs.shape[1]
    gain = norm_gain[0]
    total_features = out_cols * row_count
    received = jnp.zeros((rows, pieces), jnp.float32)
    results = jnp.zeros((micro, rows, pieces), jnp.float32)
    for step in range(micro + 1):
        fresh = inputs[min(step, micro - 1)]
        earlier = inputs[max(step - 1, 0)]
        current = jnp.where(section_id == 0, fresh, earlier + received)
        first, second = split_two(lax.all_gather(current, "row", axis=1, tiled=True))
        double = jnp.concatenate([first, second], axis=0)
        prod_one = jnp.dot(double, wfirst, preferred_element_type=jnp.float32)
        prod_two = jnp.dot(first, wsecond, preferred_element_type=jnp.float32)
        partial_value = prod_one[:rows] + prod_one[rows:] + prod_two
        summed = lax.psum_scatter(partial_value, "col", scatter_dimension=1, tiled=True)
        active = jax.nn.gelu(summed, approximate=True)
        squares = lax.psum(jnp.sum(active * active, axis=1), ("row", "col"))
        scale = lax.rsqrt(squares / total_features + 1e-06)
        normed = active * scale[:, None] * gain[None, :]
        position = step - section_id
        valid = jnp.logical_and(position >= 0, position < micro)
        place = jnp.clip(position, 0, micro - 1)
        former = lax.dynamic_index_in_dim(results, place, 0, keepdims=False)
        results = lax.dynamic_update_index_in_dim(
            results, jnp.where(valid, normed, former), place, 0
        )
        if step < micro:
            received = from_behind(normed, "section", 1)
    return results[None]


def solution(mesh):
    placed = (
        P(None, None, ("row", "col")),
        P("section", None, "col", None, "row"),
        P("section", ("row", "col")),
    )
    return jax.shard_map(
        shards,
        mesh=mesh,
        in_specs=placed,
        out_specs=P("section", None, None, ("row", "col")),
        check_vma=False,
    )
```

profile of v0, /device:TPU:0, one launch (start us, length us, event | category | flops | bytes accessed | tf_op | source)
XLA Modules:
  0.0 658.9 jit_solution(15960127548872160041)
XLA Ops:
  6.5 1.9 slice.38
  8.5 32.8 %bitcast_convert_fusion = bf16[4096,4096]{1,0:T(8,128)(2,1)} fusion(f32[1,4,1,1024,4096]{4,3,2,1,0:T(8,128)} %param.4), kind=kLoop, calls=%fused_computation.1 | loop fusion | flops 16777216 | bytes 100663296 | tf_op jit(solution)/shard_map/convert_element_type | solution.py:14
  41.3 42.3 %fusion = bf16[4096,4096]{1,0:T(8,128)(2,1)} fusion(f32[1,4,1,1024,4096]{4,3,2,1,0:T(8,128)} %param.4, bf16[4096,4096]{1,0:T(8,128)(2,1)} %bitcast_convert_fusion), kind=kLoop, calls=%fused_computation.2 | loop fusion | flops 50331648 | bytes 134217728 | tf_op jit(solution)/shard_map/convert_element_type | solution.py:15
  86.1 15.1 %fusion.2 = f32[256,4096]{1,0:T(8,128)S(1)} fusion(bf16[4096,4096]{1,0:T(8,128)(2,1)} %bitcast_convert_fusion, bf16[128,4096]{1,0:T(8,128)(2,1)S(1)} %fusion.18, bf16[128,4096]{1,0:T(8,128)(2,1)S(1)} %bitcast_convert_fusion.1), kind=kOutput, calls=%fused_computation.12 | convolution fusion | flops 8594128896 | bytes 39845888 | tf_op jit(solution)/shard_map/dot_general | solution.py:38
  101.2 16.6 %fusion.1 = f32[128,4096]{1,0:T(8,128)} fusion(bf16[128,4096]{1,0:T(8,128)(2,1)S(1)} %bitcast_convert_fusion.1, bf16[4096,4096]{1,0:T(8,128)(2,1)} %fusion, f32[256,4096]{1,0:T(8,128)S(1)} %fusion.2), kind=kOutput, calls=%fused_computation.4 | convolution fusion | flops 4296015872 | bytes 40894464 | tf_op jit(solution)/shard_map/dot_general | solution.py:39
  117.9 46.5 %reduce-scatter.5.cloned.1.call-done = f32[128,1024]{1,0:T(8,128)} async-done(((f32[128,4096]{1,0:T(8,128)}), f32[128,1024]{1,0:T(8,128)}) %reduce-scatter.5.cloned.1.call-update) | async-done | bytes 524304 | tf_op jit(solution)/shard_map/reduce_scatter | solution.py:41
  165.7 31.4 %psum.28 = f32[128]{0:T(128)S(1)} all-reduce(f32[128]{0:T(128)S(1)} %multiply_reduce_fusion.3), channel_id=1, replica_groups=mesh['section'=2,'row'=4,'col'=4] {'row','col'}, use_global_device_ids=true, to_apply=%region_2.3 | all-reduce | flops 128 | bytes 1024 | tf_op jit(solution)/shard_map/psum | solution.py:43
  197.4 2.1 bitcast_dynamic-update-slice_fusion.3
  199.4 4.2 collective-permute-start
  203.6 7.8 %collective-permute-done = f32[128,1024]{1,0:T(8,128)} collective-permute-done((f32[128,1024]{1,0:T(8,128)}, f32[128,1024]{1,0:T(8,128)}, u32[]{:S(2)}, u32[]{:S(2)}) %collective-permute-start) | collective-permute-done | bytes 524320 | tf_op jit(solution)/shard_map/ppermute | solution.py:10
  211.4 1.9 fusion.47
  213.6 23.1 %all-gather.6.cloned.1.call-done = f32[128,4096]{1,0:T(8,128)} async-done(((f32[128,1024]{1,0:T(8,128)}), f32[128,4096]{1,0:T(8,128)}) %all-gather.6.cloned.1.call-update) | async-done | bytes 2097168 | tf_op jit(solution)/shard_map/all_gather | solution.py:36
  236.7 1.9 convert_element_type.51
  239.1 16.1 %fusion.6 = f32[256,4096]{1,0:T(8,128)} fusion(bf16[4096,4096]{1,0:T(8,128)(2,1)} %bitcast_convert_fusion, bf16[128,4096]{1,0:T(8,128)(2,1)S(1)} %subtract_convert_fusion.2, bf16[128,4096]{1,0:T(8,128)(2,1)S(1)} %convert_element_type.51), kind=kOutput, calls=%fused_computation.16 | convolution fusion | flops 8594128896 | bytes 39845888 | tf_op jit(solution)/shard_map/dot_general | solution.py:38
  255.2 17.8 %convolution_add_fusion.2 = f32[128,4096]{1,0:T(8,128)} fusion(bf16[128,4096]{1,0:T(8,128)(2,1)S(1)} %convert_element_type.51, bf16[4096,4096]{1,0:T(8,128)(2,1)} %fusion, f32[256,4096]{1,0:T(8,128)} %fusion.6), kind=kOutput, calls=%fused_computation.7 | convolution fusion | flops 4296015872 | bytes 40894464 | tf_op jit(solution)/shard_map/dot_general | solution.py:39
  273.9 42.9 %reduce-scatter.7.cloned.1.call-done = f32[128,1024]{1,0:T(8,128)} async-done(((f32[128,4096]{1,0:T(8,128)}), f32[128,1024]{1,0:T(8,128)}) %reduce-scatter.7.cloned.1.call-update) | async-done | bytes 524304 | tf_op jit(solution)/shard_map/reduce_scatter | solution.py:41
  318.1 31.4 %psum.29 = f32[128]{0:T(128)S(1)} all-reduce(f32[128]{0:T(128)S(1)} %multiply_reduce_fusion.2), channel_id=1, replica_groups=mesh['section'=2,'row'=4,'col'=4] {'row','col'}, use_global_device_ids=true, to_apply=%region_5.6 | all-reduce | flops 128 | bytes 1024 | tf_op jit(solution)/shard_map/psum | solution.py:43
  351.0 3.4 collective-permute-start.1
  354.4 8.3 %collective-permute-done.1 = f32[128,1024]{1,0:T(8,128)S(1)} collective-permute-done((f32[128,1024]{1,0:T(8,128)S(1)}, f32[128,1024]{1,0:T(8,128)S(1)}, u32[]{:S(2)}, u32[]{:S(2)}) %collective-permute-start.1) | collective-permute-done | bytes 524320 | tf_op jit(solution)/shard_map/ppermute | solution.py:10
  363.9 23.0 %all-gather.8.cloned.1.call-done = f32[128,4096]{1,0:T(8,128)} async-done(((f32[128,1024]{1,0:T(8,128)}), f32[128,4096]{1,0:T(8,128)}) %all-gather.8.cloned.1.call-update) | async-done | bytes 2097168 | tf_op jit(solution)/shard_map/all_gather | solution.py:36
  389.3 16.1 %fusion.10 = f32[256,4096]{1,0:T(8,128)} fusion(bf16[4096,4096]{1,0:T(8,128)(2,1)} %bitcast_convert_fusion, bf16[128,4096]{1,0:T(8,128)(2,1)S(1)} %subtract_convert_fusion.1, bf16[128,4096]{1,0:T(8,128)(2,1)S(1)} %convert_element_type.54), kind=kOutput, calls=%fused_computation.20 | convolution fusion | flops 8594128896 | bytes 39845888 | tf_op jit(solution)/shard_map/dot_general | solution.py:38
  405.4 17.8 %convolution_add_fusion.1 = f32[128,4096]{1,0:T(8,128)} fusion(bf16[128,4096]{1,0:T(8,128)(2,1)S(1)} %convert_element_type.54, bf16[4096,4096]{1,0:T(8,128)(2,1)} %fusion, f32[256,4096]{1,0:T(8,128)} %fusion.10), kind=kOutput, calls=%fused_computation.6 | convolution fusion | flops 4296015872 | bytes 40894464 | tf_op jit(solution)/shard_map/dot_general | solution.py:39
  424.1 42.9 %reduce-scatter.9.cloned.1.call-done = f32[128,1024]{1,0:T(8,128)} async-done(((f32[128,4096]{1,0:T(8,128)}), f32[128,1024]{1,0:T(8,128)}) %reduce-scatter.9.cloned.1.call-update) | async-done | bytes 524304 | tf_op jit(solution)/shard_map/reduce_scatter | solution.py:41
  468.4 31.4 %psum.30 = f32[128]{0:T(128)S(1)} all-reduce(f32[128]{0:T(128)S(1)} %multiply_reduce_fusion.1), channel_id=1, replica_groups=mesh['section'=2,'row'=4,'col'=4] {'row','col'}, use_global_device_ids=true, to_apply=%region_8.9 | all-reduce | flops 128 | bytes 1024 | tf_op jit(solution)/shard_map/psum | solution.py:43
  501.2 3.4 collective-permute-start.2
  504.6 8.3 %collective-permute-done.2 = f32[128,1024]{1,0:T(8,128)S(1)} collective-permute-done((f32[128,1024]{1,0:T(8,128)S(1)}, f32[128,1024]{1,0:T(8,128)S(1)}, u32[]{:S(2)}, u32[]{:S(2)}) %collective-permute-start.2) | collective-permute-done | bytes 524320 | tf_op jit(solution)/shard_map/ppermute | solution.py:10
  514.1 23.0 %all-gather.10.cloned.1.call-done = f32[128,4096]{1,0:T(8,128)} async-done(((f32[128,1024]{1,0:T(8,128)}), f32[128,4096]{1,0:T(8,128)}) %all-gather.10.cloned.1.call-update) | async-done | bytes 2097168 | tf_op jit(solution)/shard_map/all_gather | solution.py:36
  539.6 16.1 %fusion.14 = f32[256,4096]{1,0:T(8,128)} fusion(bf16[4096,4096]{1,0:T(8,128)(2,1)} %bitcast_convert_fusion, bf16[128,4096]{1,0:T(8,128)(2,1)S(1)} %subtract_convert_fusion, bf16[128,4096]{1,0:T(8,128)(2,1)S(1)} %convert_element_type.57), kind=kOutput, calls=%fused_computation.24 | convolution fusion | flops 8594128896 | bytes 39845888 | tf_op jit(solution)/shard_map/dot_general | solution.py:38
  555.7 17.8 %convolution_add_fusion = f32[128,4096]{1,0:T(8,128)} fusion(bf16[128,4096]{1,0:T(8,128)(2,1)S(1)} %convert_element_type.57, bf16[4096,4096]{1,0:T(8,128)(2,1)} %fusion, f32[256,4096]{1,0:T(8,128)} %fusion.14), kind=kOutput, calls=%fused_computation.5 | convolution fusion | flops 4296015872 | bytes 40894464 | tf_op jit(solution)/shard_map/dot_general | solution.py:39
  574.6 42.6 %reduce-scatter.11.cloned.1.call-done = f32[128,1024]{1,0:T(8,128)} async-done(((f32[128,4096]{1,0:T(8,128)}), f32[128,1024]{1,0:T(8,128)}) %reduce-scatter.11.cloned.1.call-update) | async-done | bytes 524304 | tf_op jit(solution)/shard_map/reduce_scatter | solution.py:41
  618.6 31.4 %psum.31 = f32[128]{0:T(128)S(1)} all-reduce(f32[128]{0:T(128)S(1)} %multiply_reduce_fusion), channel_id=1, replica_groups=mesh['section'=2,'row'=4,'col'=4] {'row','col'}, use_global_device_ids=true, to_apply=%region_11.12 | all-reduce | flops 128 | bytes 1024 | tf_op jit(solution)/shard_map/psum | solution.py:43
  650.0 2.1 bitcast_dynamic-update-slice_fusion
  (52 shorter events, 21.9 us)
Async XLA Ops:
  6.5 77.1 %all-gather.12.cloned.1.call-start = ((), (), s32[]{:S(2)}) async-start(), calls=%async_computation.11 | async-start | bytes 2621440 | tf_op jit(solution)/shard_map/all_gather | solution.py:36
  8.4 156.0 %reduce-scatter.5.cloned.1.call-start = ((), (), s32[]{:S(2)}) async-start(), calls=%async_computation.4 | async-start | bytes 2621440 | tf_op jit(solution)/shard_map/reduce_scatter | solution.py:41
  83.6 2.2 copy-start
  117.8 79.5 %copy-start.5 = (f32[1,1024]{1,0:T(1,128)S(1)}, f32[1,1024]{1,0:T(1,128)}, u32[]{:S(2)}) copy-start(f32[1,1024]{1,0:T(1,128)} %param.5) | copy-start | bytes 12292
  117.8 93.6 %copy-start.4 = (f32[3,128,1024]{2,1,0:T(8,128)S(1)}, f32[3,128,1024]{2,1,0:T(8,128)}, u32[]{:S(2)}) copy-start(f32[3,128,1024]{2,1,0:T(8,128)} %param.3) | copy-start | bytes 4718596
  117.9 118.8 %all-gather.6.cloned.1.call-start = ((), (), s32[]{:S(2)}) async-start(), calls=%async_computation.5 | async-start | bytes 2621440 | tf_op jit(solution)/shard_map/all_gather | solution.py:36
  199.4 12.0 %collective-permute-start = (f32[128,1024]{1,0:T(8,128)}, f32[128,1024]{1,0:T(8,128)}, u32[]{:S(2)}, u32[]{:S(2)}) collective-permute-start(f32[128,1024]{1,0:T(8,128)} %get-tuple-element.10), channel_id=1, source_target_pairs={{0,16},{1,17},{2,18},{3,19},{4,20},{5,21},{6,22},{7,23},{8,24},{9,... | collective-permute-start | bytes 1572872 | tf_op jit(solution)/shard_map/ppermute | solution.py:10
  213.4 103.4 %reduce-scatter.7.cloned.1.call-start = ((), (), s32[]{:S(2)}) async-start(), calls=%async_computation.6 | async-start | bytes 2621440 | tf_op jit(solution)/shard_map/reduce_scatter | solution.py:41
  236.7 2.2 copy-start.1
  273.0 113.9 %all-gather.8.cloned.1.call-start = ((), (), s32[]{:S(2)}) async-start(), calls=%async_computation.7 | async-start | bytes 2621440 | tf_op jit(solution)/shard_map/all_gather | solution.py:36
  351.0 11.7 %collective-permute-start.1 = (f32[128,1024]{1,0:T(8,128)S(1)}, f32[128,1024]{1,0:T(8,128)S(1)}, u32[]{:S(2)}, u32[]{:S(2)}) collective-permute-start(f32[128,1024]{1,0:T(8,128)S(1)} %get-tuple-element.8), channel_id=1, source_target_pairs={{0,16},{1,17},{2,18},{3,19},{4,20},{5,21},{6,22},{7,23},{8,24},{9,... | collective-permute-start | bytes 1572872 | tf_op jit(solution)/shard_map/ppermute | solution.py:10
  363.6 103.4 %reduce-scatter.9.cloned.1.call-start = ((), (), s32[]{:S(2)}) async-start(), calls=%async_computation.8 | async-start | bytes 2621440 | tf_op jit(solution)/shard_map/reduce_scatter | solution.py:41
  386.9 2.2 copy-start.2
  423.3 113.8 %all-gather.10.cloned.1.call-start = ((), (), s32[]{:S(2)}) async-start(), calls=%async_computation.9 | async-start | bytes 2621440 | tf_op jit(solution)/shard_map/all_gather | solution.py:36
  501.2 11.7 %collective-permute-start.2 = (f32[128,1024]{1,0:T(8,128)S(1)}, f32[128,1024]{1,0:T(8,128)S(1)}, u32[]{:S(2)}, u32[]{:S(2)}) collective-permute-start(f32[128,1024]{1,0:T(8,128)S(1)} %get-tuple-element.6), channel_id=1, source_target_pairs={{0,16},{1,17},{2,18},{3,19},{4,20},{5,21},{6,22},{7,23},{8,24},{9,... | collective-permute-start | bytes 1572872 | tf_op jit(solution)/shard_map/ppermute | solution.py:10
  513.8 103.4 %reduce-scatter.11.cloned.1.call-start = ((), (), s32[]{:S(2)}) async-start(), calls=%async_computation.10 | async-start | bytes 2621440 | tf_op jit(solution)/shard_map/reduce_scatter | solution.py:41
  537.1 2.2 copy-start.3
Sparse Core Ops, SparseCore 0:
  8.9 25.2 all-gather.11
  118.0 46.3 reduce-scatter.4
  213.5 23.1 all-gather.5
  273.2 43.6 reduce-scatter.6
  363.7 23.0 all-gather.7
  423.4 43.6 reduce-scatter.8
  514.0 23.0 all-gather.9
  573.6 43.6 reduce-scatter.10
where the time goes:
time: 660 us; the launch traced here: 659 us
  waiting for transfers between devices  268 us (41%)
  matrix products  133 us (20%)
  blocking collectives  126 us (19%)
  other arithmetic  99.4 us (15%)
  between operations  13.7 us (2%)
  starting transfers between devices  12 us (2%)
    reduce_scatter x4, waiting for transfers between devices, shards(): lax.psum_scatter(partial_value, 'col', scatter_dimension=1, tiled=True)  175 us
    psum x4, blocking collectives, shards(): squares = lax.psum(jnp.sum(active * active, axis=1), ('row', 'col'))  126 us
    dot_general x4, matrix products, shards(): prod_two = jnp.dot(first, wsecond, preferred_element_type=jnp.float32)  70 us
    all_gather x4, waiting for transfers between devices, shards(): lax.all_gather(current, 'row', axis=1, tiled=True)  69 us
    dot_general x4, matrix products, shards(): prod_one = jnp.dot(double, wfirst, preferred_element_type=jnp.float32)  63.4 us
    convert_element_type x5, other arithmetic, split_two(): (values - first.astype(jnp.float32)).astype(jnp.bfloat16)  43.2 us
    convert_element_type x5, other arithmetic, split_two(): first = lax.optimization_barrier(values.astype(jnp.bfloat16))  40.2 us
    ppermute x3, waiting for transfers between devices, from_behind(): lax.ppermute(value, axis, [(source, source + steps) for source in range(i...  24.4 us
  transfers between devices with their start and end apart: 11, of which 10 were waited for; matrix products, arithmetic and copies ran while one was open for 12% of the time, Pallas kernels for 0%

commit v1 on v0

--- a/solution.py
+++ b/solution.py
@@ -40,7 +40,7 @@
         partial_value = prod_one[:rows] + prod_one[rows:] + prod_two
         summed = lax.psum_scatter(partial_value, "col", scatter_dimension=1, tiled=True)
         active = jax.nn.gelu(summed, approximate=True)
-        squares = lax.psum(jnp.sum(active * active, axis=1), ("row", "col"))
+        squares = lax.psum(lax.psum(jnp.sum(active * active, axis=1), "row"), "col")
         scale = lax.rsqrt(squares / total_features + 1e-06)
         normed = active * scale[:, None] * gain[None, :]
         position = step - section_id

time: 660 us -> 596 us (0.903)
  blocking collectives: 126 us -> 65.4 us
    psum x4 -> x8, blocking collectives: 126 us -> 65.4 us  [shards(): squares = lax.psum(lax.psum(jnp.sum(active * active, axis=1), 'row'), 'col')]
  transfers between devices with their start and end apart: 11 -> 11, of which waited for: 10 -> 10; matrix products, arithmetic and copies ran while one was open for 12% -> 13% of each run, Pallas kernels for 0% -> 0%
where the time goes in v1:
time: 596 us; the launch traced here: 595 us
  waiting for transfers between devices  265 us (44%)
  matrix products  134 us (22%)
  other arithmetic  99.4 us (17%)
  blocking collectives  65.4 us (11%)
  between operations  13.7 us (2%)
  starting transfers between devices  12 us (2%)
  local copies, waits for them, and re-layouts  6.28 us (1%)
    reduce_scatter x4, waiting for transfers between devices, shards(): lax.psum_scatter(partial_value, 'col', scatter_dimension=1, tiled=True)  175 us
    dot_general x4, matrix products, shards(): prod_two = jnp.dot(first, wsecond, preferred_element_type=jnp.float32)  70 us
    psum x8, blocking collectives, shards(): squares = lax.psum(lax.psum(jnp.sum(active * active, axis=1), 'row'), 'col')  65.4 us
    all_gather x4, waiting for transfers between devices, shards(): lax.all_gather(current, 'row', axis=1, tiled=True)  65.3 us
    dot_general x4, matrix products, shards(): prod_one = jnp.dot(double, wfirst, preferred_element_type=jnp.float32)  63.6 us
    convert_element_type x5, other arithmetic, split_two(): (values - first.astype(jnp.float32)).astype(jnp.bfloat16)  43.3 us
    convert_element_type x5, other arithmetic, split_two(): first = lax.optimization_barrier(values.astype(jnp.bfloat16))  40.2 us
    ppermute x3, waiting for transfers between devices, from_behind(): lax.ppermute(value, axis, [(source, source + steps) for source in range(i...  24.7 us
  transfers between devices with their start and end apart: 11, of which 10 were waited for; matrix products, arithmetic and copies ran while one was open for 13% of the time, Pallas kernels for 0%

profile of v1, /device:TPU:0, one launch (start us, length us, event | category | flops | bytes accessed | tf_op | source)
XLA Modules:
  0.0 595.4 jit_solution(7304715233619528585)
XLA Ops:
  8.5 32.8 %bitcast_convert_fusion = bf16[4096,4096]{1,0:T(8,128)(2,1)} fusion(f32[1,4,1,1024,4096]{4,3,2,1,0:T(8,128)} %param.4), kind=kLoop, calls=%fused_computation.1 | loop fusion | flops 16777216 | bytes 100663296 | tf_op jit(solution)/shard_map/convert_element_type | solution.py:14
  41.3 42.3 %fusion = bf16[4096,4096]{1,0:T(8,128)(2,1)} fusion(f32[1,4,1,1024,4096]{4,3,2,1,0:T(8,128)} %param.4, bf16[4096,4096]{1,0:T(8,128)(2,1)} %bitcast_convert_fusion), kind=kLoop, calls=%fused_computation.2 | loop fusion | flops 50331648 | bytes 134217728 | tf_op jit(solution)/shard_map/convert_element_type | solution.py:15
  86.1 15.1 %fusion.2 = f32[256,4096]{1,0:T(8,128)S(1)} fusion(bf16[4096,4096]{1,0:T(8,128)(2,1)} %bitcast_convert_fusion, bf16[128,4096]{1,0:T(8,128)(2,1)S(1)} %fusion.18, bf16[128,4096]{1,0:T(8,128)(2,1)S(1)} %bitcast_convert_fusion.1), kind=kOutput, calls=%fused_computation.12 | convolution fusion | flops 8594128896 | bytes 39845888 | tf_op jit(solution)/shard_map/dot_general | solution.py:38
  101.2 16.7 %fusion.1 = f32[128,4096]{1,0:T(8,128)} fusion(bf16[128,4096]{1,0:T(8,128)(2,1)S(1)} %bitcast_convert_fusion.1, bf16[4096,4096]{1,0:T(8,128)(2,1)} %fusion, f32[256,4096]{1,0:T(8,128)S(1)} %fusion.2), kind=kOutput, calls=%fused_computation.4 | convolution fusion | flops 4296015872 | bytes 40894464 | tf_op jit(solution)/shard_map/dot_general | solution.py:39
  118.0 46.5 %reduce-scatter.5.cloned.1.call-done = f32[128,1024]{1,0:T(8,128)} async-done(((f32[128,4096]{1,0:T(8,128)}), f32[128,1024]{1,0:T(8,128)}) %reduce-scatter.5.cloned.1.call-update) | async-done | bytes 524304 | tf_op jit(solution)/shard_map/reduce_scatter | solution.py:41
  165.8 6.1 %psum.56 = f32[128]{0:T(128)S(1)} all-reduce(f32[128]{0:T(128)S(1)} %multiply_reduce_fusion.3), channel_id=1, replica_groups=mesh['section'=2,'row'=4,'col'=4] {'row'}, use_global_device_ids=true, to_apply=%region_2.3 | all-reduce | flops 128 | bytes 1024 | tf_op jit(solution)/shard_map/psum | solution.py:43
  172.0 10.2 %psum.57 = f32[128]{0:T(128)S(1)} all-reduce(f32[128]{0:T(128)S(1)} %psum.56), channel_id=1, replica_groups=mesh['section'=2,'row'=4,'col'=4] {'col'}, use_global_device_ids=true, to_apply=%region_3.4 | all-reduce | flops 128 | bytes 1024 | tf_op jit(solution)/shard_map/psum | solution.py:43
  182.4 2.1 bitcast_dynamic-update-slice_fusion.3
  184.4 4.2 collective-permute-start
  188.6 7.9 %collective-permute-done = f32[128,1024]{1,0:T(8,128)} collective-permute-done((f32[128,1024]{1,0:T(8,128)}, f32[128,1024]{1,0:T(8,128)}, u32[]{:S(2)}, u32[]{:S(2)}) %collective-permute-start) | collective-permute-done | bytes 524320 | tf_op jit(solution)/shard_map/ppermute | solution.py:10
  198.7 21.8 %all-gather.6.cloned.1.call-done = f32[128,4096]{1,0:T(8,128)} async-done(((f32[128,1024]{1,0:T(8,128)}), f32[128,4096]{1,0:T(8,128)}) %all-gather.6.cloned.1.call-update) | async-done | bytes 2097168 | tf_op jit(solution)/shard_map/all_gather | solution.py:36
  223.0 16.1 %fusion.6 = f32[256,4096]{1,0:T(8,128)} fusion(bf16[4096,4096]{1,0:T(8,128)(2,1)} %bitcast_convert_fusion, bf16[128,4096]{1,0:T(8,128)(2,1)S(1)} %subtract_convert_fusion.2, bf16[128,4096]{1,0:T(8,128)(2,1)S(1)} %convert_element_type.51), kind=kOutput, calls=%fused_computation.16 | convolution fusion | flops 8594128896 | bytes 39845888 | tf_op jit(solution)/shard_map/dot_general | solution.py:38
  239.2 17.8 %convolution_add_fusion.2 = f32[128,4096]{1,0:T(8,128)} fusion(bf16[128,4096]{1,0:T(8,128)(2,1)S(1)} %convert_element_type.51, bf16[4096,4096]{1,0:T(8,128)(2,1)} %fusion, f32[256,4096]{1,0:T(8,128)} %fusion.6), kind=kOutput, calls=%fused_computation.7 | convolution fusion | flops 4296015872 | bytes 40894464 | tf_op jit(solution)/shard_map/dot_general | solution.py:39
  257.9 42.9 %reduce-scatter.7.cloned.1.call-done = f32[128,1024]{1,0:T(8,128)} async-done(((f32[128,4096]{1,0:T(8,128)}), f32[128,1024]{1,0:T(8,128)}) %reduce-scatter.7.cloned.1.call-update) | async-done | bytes 524304 | tf_op jit(solution)/shard_map/reduce_scatter | solution.py:41
  302.1 6.1 %psum.58 = f32[128]{0:T(128)S(1)} all-reduce(f32[128]{0:T(128)S(1)} %multiply_reduce_fusion.2), channel_id=1, replica_groups=mesh['section'=2,'row'=4,'col'=4] {'row'}, use_global_device_ids=true, to_apply=%region_6.7 | all-reduce | flops 128 | bytes 1024 | tf_op jit(solution)/shard_map/psum | solution.py:43
  308.2 10.2 %psum.59 = f32[128]{0:T(128)S(1)} all-reduce(f32[128]{0:T(128)S(1)} %psum.58), channel_id=1, replica_groups=mesh['section'=2,'row'=4,'col'=4] {'col'}, use_global_device_ids=true, to_apply=%region_7.8 | all-reduce | flops 128 | bytes 1024 | tf_op jit(solution)/shard_map/psum | solution.py:43
  319.9 3.4 collective-permute-start.1
  323.3 8.4 %collective-permute-done.1 = f32[128,1024]{1,0:T(8,128)S(1)} collective-permute-done((f32[128,1024]{1,0:T(8,128)S(1)}, f32[128,1024]{1,0:T(8,128)S(1)}, u32[]{:S(2)}, u32[]{:S(2)}) %collective-permute-start.1) | collective-permute-done | bytes 524320 | tf_op jit(solution)/shard_map/ppermute | solution.py:10
  332.8 21.8 %all-gather.8.cloned.1.call-done = f32[128,4096]{1,0:T(8,128)} async-done(((f32[128,1024]{1,0:T(8,128)}), f32[128,4096]{1,0:T(8,128)}) %all-gather.8.cloned.1.call-update) | async-done | bytes 2097168 | tf_op jit(solution)/shard_map/all_gather | solution.py:36
  357.1 16.1 %fusion.10 = f32[256,4096]{1,0:T(8,128)} fusion(bf16[4096,4096]{1,0:T(8,128)(2,1)} %bitcast_convert_fusion, bf16[128,4096]{1,0:T(8,128)(2,1)S(1)} %subtract_convert_fusion.1, bf16[128,4096]{1,0:T(8,128)(2,1)S(1)} %convert_element_type.54), kind=kOutput, calls=%fused_computation.20 | convolution fusion | flops 8594128896 | bytes 39845888 | tf_op jit(solution)/shard_map/dot_general | solution.py:38
  373.2 17.8 %convolution_add_fusion.1 = f32[128,4096]{1,0:T(8,128)} fusion(bf16[128,4096]{1,0:T(8,128)(2,1)S(1)} %convert_element_type.54, bf16[4096,4096]{1,0:T(8,128)(2,1)} %fusion, f32[256,4096]{1,0:T(8,128)} %fusion.10), kind=kOutput, calls=%fused_computation.6 | convolution fusion | flops 4296015872 | bytes 40894464 | tf_op jit(solution)/shard_map/dot_general | solution.py:39
  391.9 42.9 %reduce-scatter.9.cloned.1.call-done = f32[128,1024]{1,0:T(8,128)} async-done(((f32[128,4096]{1,0:T(8,128)}), f32[128,1024]{1,0:T(8,128)}) %reduce-scatter.9.cloned.1.call-update) | async-done | bytes 524304 | tf_op jit(solution)/shard_map/reduce_scatter | solution.py:41
  436.1 6.2 %psum.60 = f32[128]{0:T(128)S(1)} all-reduce(f32[128]{0:T(128)S(1)} %multiply_reduce_fusion.1), channel_id=1, replica_groups=mesh['section'=2,'row'=4,'col'=4] {'row'}, use_global_device_ids=true, to_apply=%region_10.11 | all-reduce | flops 128 | bytes 1024 | tf_op jit(solution)/shard_map/psum | solution.py:43
  442.3 10.2 %psum.61 = f32[128]{0:T(128)S(1)} all-reduce(f32[128]{0:T(128)S(1)} %psum.60), channel_id=1, replica_groups=mesh['section'=2,'row'=4,'col'=4] {'col'}, use_global_device_ids=true, to_apply=%region_11.12 | all-reduce | flops 128 | bytes 1024 | tf_op jit(solution)/shard_map/psum | solution.py:43
  453.9 3.4 collective-permute-start.2
  457.3 8.4 %collective-permute-done.2 = f32[128,1024]{1,0:T(8,128)S(1)} collective-permute-done((f32[128,1024]{1,0:T(8,128)S(1)}, f32[128,1024]{1,0:T(8,128)S(1)}, u32[]{:S(2)}, u32[]{:S(2)}) %collective-permute-start.2) | collective-permute-done | bytes 524320 | tf_op jit(solution)/shard_map/ppermute | solution.py:10
  466.9 21.7 %all-gather.10.cloned.1.call-done = f32[128,4096]{1,0:T(8,128)} async-done(((f32[128,1024]{1,0:T(8,128)}), f32[128,4096]{1,0:T(8,128)}) %all-gather.10.cloned.1.call-update) | async-done | bytes 2097168 | tf_op jit(solution)/shard_map/all_gather | solution.py:36
  491.1 16.2 %fusion.14 = f32[256,4096]{1,0:T(8,128)} fusion(bf16[4096,4096]{1,0:T(8,128)(2,1)} %bitcast_convert_fusion, bf16[128,4096]{1,0:T(8,128)(2,1)S(1)} %subtract_convert_fusion, bf16[128,4096]{1,0:T(8,128)(2,1)S(1)} %convert_element_type.57), kind=kOutput, calls=%fused_computation.24 | convolution fusion | flops 8594128896 | bytes 39845888 | tf_op jit(solution)/shard_map/dot_general | solution.py:38
  507.2 17.8 %convolution_add_fusion = f32[128,4096]{1,0:T(8,128)} fusion(bf16[128,4096]{1,0:T(8,128)(2,1)S(1)} %convert_element_type.57, bf16[4096,4096]{1,0:T(8,128)(2,1)} %fusion, f32[256,4096]{1,0:T(8,128)} %fusion.14), kind=kOutput, calls=%fused_computation.5 | convolution fusion | flops 4296015872 | bytes 40894464 | tf_op jit(solution)/shard_map/dot_general | solution.py:39
  526.2 42.6 %reduce-scatter.11.cloned.1.call-done = f32[128,1024]{1,0:T(8,128)} async-done(((f32[128,4096]{1,0:T(8,128)}), f32[128,1024]{1,0:T(8,128)}) %reduce-scatter.11.cloned.1.call-update) | async-done | bytes 524304 | tf_op jit(solution)/shard_map/reduce_scatter | solution.py:41
  570.1 6.2 %psum.62 = f32[128]{0:T(128)S(1)} all-reduce(f32[128]{0:T(128)S(1)} %multiply_reduce_fusion), channel_id=1, replica_groups=mesh['section'=2,'row'=4,'col'=4] {'row'}, use_global_device_ids=true, to_apply=%region_14.15 | all-reduce | flops 128 | bytes 1024 | tf_op jit(solution)/shard_map/psum | solution.py:43
  576.3 10.2 %psum.63 = f32[128]{0:T(128)S(1)} all-reduce(f32[128]{0:T(128)S(1)} %psum.62), channel_id=1, replica_groups=mesh['section'=2,'row'=4,'col'=4] {'col'}, use_global_device_ids=true, to_apply=%region_15.16 | all-reduce | flops 128 | bytes 1024 | tf_op jit(solution)/shard_map/psum | solution.py:43
  (56 shorter events, 29.6 us)
Async XLA Ops:
  6.5 77.1 %all-gather.12.cloned.1.call-start = ((), (), s32[]{:S(2)}) async-start(), calls=%async_computation.11 | async-start | bytes 2621440 | tf_op jit(solution)/shard_map/all_gather | solution.py:36
  8.4 156.1 %reduce-scatter.5.cloned.1.call-start = ((), (), s32[]{:S(2)}) async-start(), calls=%async_computation.4 | async-start | bytes 2621440 | tf_op jit(solution)/shard_map/reduce_scatter | solution.py:41
  83.6 2.2 copy-start
  117.9 64.5 %copy-start.5 = (f32[1,1024]{1,0:T(1,128)S(1)}, f32[1,1024]{1,0:T(1,128)}, u32[]{:S(2)}) copy-start(f32[1,1024]{1,0:T(1,128)} %param.5) | copy-start | bytes 12292
  117.9 78.6 %copy-start.4 = (f32[3,128,1024]{2,1,0:T(8,128)S(1)}, f32[3,128,1024]{2,1,0:T(8,128)}, u32[]{:S(2)}) copy-start(f32[3,128,1024]{2,1,0:T(8,128)} %param.3) | copy-start | bytes 4718596
  118.0 102.6 %all-gather.6.cloned.1.call-start = ((), (), s32[]{:S(2)}) async-start(), calls=%async_computation.5 | async-start | bytes 2621440 | tf_op jit(solution)/shard_map/all_gather | solution.py:36
  184.4 12.1 %collective-permute-start = (f32[128,1024]{1,0:T(8,128)}, f32[128,1024]{1,0:T(8,128)}, u32[]{:S(2)}, u32[]{:S(2)}) collective-permute-start(f32[128,1024]{1,0:T(8,128)} %get-tuple-element.10), channel_id=1, source_target_pairs={{0,16},{1,17},{2,18},{3,19},{4,20},{5,21},{6,22},{7,23},{8,24},{9,... | collective-permute-start | bytes 1572872 | tf_op jit(solution)/shard_map/ppermute | solution.py:10
  198.5 102.3 %reduce-scatter.7.cloned.1.call-start = ((), (), s32[]{:S(2)}) async-start(), calls=%async_computation.6 | async-start | bytes 2621440 | tf_op jit(solution)/shard_map/reduce_scatter | solution.py:41
  220.6 2.2 copy-start.1
  257.0 97.6 %all-gather.8.cloned.1.call-start = ((), (), s32[]{:S(2)}) async-start(), calls=%async_computation.7 | async-start | bytes 2621440 | tf_op jit(solution)/shard_map/all_gather | solution.py:36
  319.9 11.8 %collective-permute-start.1 = (f32[128,1024]{1,0:T(8,128)S(1)}, f32[128,1024]{1,0:T(8,128)S(1)}, u32[]{:S(2)}, u32[]{:S(2)}) collective-permute-start(f32[128,1024]{1,0:T(8,128)S(1)} %get-tuple-element.8), channel_id=1, source_target_pairs={{0,16},{1,17},{2,18},{3,19},{4,20},{5,21},{6,22},{7,23},{8,24},{9,... | collective-permute-start | bytes 1572872 | tf_op jit(solution)/shard_map/ppermute | solution.py:10
  332.6 102.2 %reduce-scatter.9.cloned.1.call-start = ((), (), s32[]{:S(2)}) async-start(), calls=%async_computation.8 | async-start | bytes 2621440 | tf_op jit(solution)/shard_map/reduce_scatter | solution.py:41
  354.6 2.2 copy-start.2
  391.0 97.6 %all-gather.10.cloned.1.call-start = ((), (), s32[]{:S(2)}) async-start(), calls=%async_computation.9 | async-start | bytes 2621440 | tf_op jit(solution)/shard_map/all_gather | solution.py:36
  453.9 11.8 %collective-permute-start.2 = (f32[128,1024]{1,0:T(8,128)S(1)}, f32[128,1024]{1,0:T(8,128)S(1)}, u32[]{:S(2)}, u32[]{:S(2)}) collective-permute-start(f32[128,1024]{1,0:T(8,128)S(1)} %get-tuple-element.6), channel_id=1, source_target_pairs={{0,16},{1,17},{2,18},{3,19},{4,20},{5,21},{6,22},{7,23},{8,24},{9,... | collective-permute-start | bytes 1572872 | tf_op jit(solution)/shard_map/ppermute | solution.py:10
  466.6 102.2 %reduce-scatter.11.cloned.1.call-start = ((), (), s32[]{:S(2)}) async-start(), calls=%async_computation.10 | async-start | bytes 2621440 | tf_op jit(solution)/shard_map/reduce_scatter | solution.py:41
  488.6 2.2 copy-start.3
Sparse Core Ops, SparseCore 0:
  8.9 25.2 all-gather.11
  118.1 46.4 reduce-scatter.4
  198.6 21.8 all-gather.5
  257.1 43.6 reduce-scatter.6
  332.7 21.8 all-gather.7
  391.1 43.6 reduce-scatter.8
  466.7 21.8 all-gather.9
  525.1 43.6 reduce-scatter.10
